TPU v7x, 256 devices: a whole 4x4x8 slice. The times are simulated.
256 devices in a mesh: dp: 32 (over x, y, core), mp: 8 (over z).
Axes of the slice: x: 4, y: 4, z: 8, core: 2. Of those that a mesh axis runs over, the one named last changes fastest.
Arguments:
- vit_features: bfloat16 [128, 256, 1024], P('dp', 'mp'), may hold values from -6 to 6
- patch_counts: int32 [128], P('dp'), may hold values from 64 to 192
- text_counts: int32 [128], P('dp'), may hold values from 1 to 63
- tile_dest: int32 [128], P('dp'), may hold values from 0 to 31, as said below
- text_embeds: bfloat16 [128, 256, 4096], P('dp', 'mp'), may hold values from -6 to 6
- w_proj: bfloat16 [1024, 4096], replicated, may hold values from -0.1875 to 0.1875
- b_proj: float32 [4096], replicated, may hold values from -3 to 3
- norm_gain: float32 [1, 4096], replicated, may hold values from 0.1 to 1.9
- w_qkv: bfloat16 [1, 4096, 8, 512], P(None, 'dp', 'mp'), may hold values from -0.375 to 0.375
- w_out: bfloat16 [1, 8, 256, 4096], P(None, 'mp', None, 'dp'), may hold values from -0.125 to 0.125
Outputs:
- hidden_out: bfloat16 [128, 256, 4096], P('dp', 'mp')
Inputs may be any that keep to these rules, and one draw needn't show every extreme that they name: `tile_dest`: each language-model rank receives exactly 4 tiles; one source rank sends at most 2 tiles to one language-model rank, and every source rank sends 2 to some rank.
All inputs are finite; a program needn't handle non-finite values.
Results may differ from a plain program's by a relative error of at most 0.01.
Values may be sent and summed in bfloat16 or wider, within the bound.
No kernel may reach another device: no remote copies, remote signals or barrier semaphores. Data moves between devices by JAX's collectives and lax.ppermute only.
A program may use at most 128 MiB of HBM per device.

v0:
```python
import math
import jax
import jax.numpy as jnp
from jax import lax
from jax.sharding import PartitionSpec as P

HS = 128
GROUP = 2
CAP = 2
rope_base = 500000.0
epsilon = 1e-05


def sent_to_all(shard, axis):
    copies = jnp.broadcast_to(shard, (lax.axis_size(axis), *shard.shape))
    return lax.all_to_all(copies, axis, split_axis=0, concat_axis=0, tiled=True)


def joined_along(parts, dim):
    lengths = list(parts.shape[1:])
    lengths[dim] *= parts.shape[0]
    return jnp.moveaxis(parts, 0, dim).reshape(lengths)


def collect(shard, axis, dim):
    parts = sent_to_all(shard, axis)
    return joined_along(parts, dim)


def gather_turned(arrays, axis, dims):
    turned = [jnp.moveaxis(a, dim, 0) for a, dim in zip(arrays, dims)]
    both = jnp.concatenate([t.reshape(len(t), -1) for t in turned], axis=1)
    result, at, gathered = (lax.all_gather(both, axis, axis=0, tiled=True), 0, [])
    for t, dim in zip(turned, dims):
        section = result[:, at : at + t[0].size].reshape(-1, *t.shape[1:])
        gathered.append(jnp.moveaxis(section, 0, dim))
        at += t[0].size
    return tuple(gathered)


def tile_angles(tile_size, head_size):
    half_size = head_size // 2
    inverse = jnp.exp(
        -(2.0 * jnp.arange(half_size, dtype=jnp.float32) / head_size) * math.log(rope_base)
    )
    positions = jnp.arange(tile_size, dtype=jnp.float32)
    return positions[:, None] * inverse[None, :]


def rotate_half(values, angles):
    half_size = values.shape[-1] // 2
    cosine = jnp.cos(angles)
    sine_part = jnp.sin(angles)
    first_half = values[..., :half_size]
    second = values[..., half_size:]
    return jnp.concatenate(
        [first_half * cosine - second * sine_part, second * cosine + first_half * sine_part],
        axis=-1,
    )


def slot_table(full_dest, dest_ids):
    full_hot = (full_dest[:, None] == dest_ids[None, :]).astype(jnp.int32)
    return jnp.sum((jnp.cumsum(full_hot, axis=0) - full_hot) * full_hot, axis=1)


def send_capped(vit_features, tile_dest, own_before, full_dest, full_slots, rank_count, my_rank):
    image_count, local_rows, vision_width = vit_features.shape
    targets = tile_dest * CAP + own_before
    placing = (targets[:, None] == jnp.arange(rank_count * CAP, dtype=jnp.int32)[None, :]).astype(
        jnp.bfloat16
    )
    flat_rows = vit_features.reshape(image_count, local_rows * vision_width)
    outgoing = jnp.dot(placing.T, flat_rows, preferred_element_type=jnp.float32).astype(
        jnp.bfloat16
    )
    outgoing = outgoing.reshape(rank_count, CAP, local_rows, vision_width)
    incoming = lax.all_to_all(outgoing, "dp", split_axis=0, concat_axis=0, tiled=True)
    image_total = full_dest.shape[0]
    dest_ids = jnp.arange(rank_count, dtype=jnp.int32)
    by_source = full_dest.reshape(rank_count, image_count)
    source_hot = (by_source[:, :, None] == dest_ids[None, None, :]).astype(jnp.int32)
    source_before = jnp.sum(
        (jnp.cumsum(source_hot, axis=1) - source_hot) * source_hot, axis=2
    ).reshape(image_total)
    columns = jnp.arange(image_total, dtype=jnp.int32) // image_count * CAP + source_before
    mine_mask = full_dest == my_rank
    pick_rows = (
        mine_mask[None, :]
        & (full_slots[None, :] == jnp.arange(image_count, dtype=jnp.int32)[:, None])
    ).astype(jnp.bfloat16)
    pick_cols = (columns[:, None] == jnp.arange(rank_count * CAP, dtype=jnp.int32)[None, :]).astype(
        jnp.bfloat16
    )
    selector = jnp.dot(pick_rows, pick_cols, preferred_element_type=jnp.float32).astype(
        jnp.bfloat16
    )
    arrived = jnp.dot(
        selector,
        incoming.reshape(rank_count * CAP, local_rows * vision_width),
        preferred_element_type=jnp.float32,
    )
    return arrived.astype(jnp.bfloat16).reshape(image_count, local_rows, vision_width)


def layer_step(hidden, gain_row, weights_qkv, weights_out, lengths, angles):
    as_float = hidden.astype(jnp.float32)
    mean_square = jnp.mean(as_float * as_float, axis=-1, keepdims=True)
    normed = (as_float * lax.rsqrt(mean_square + epsilon) * gain_row).astype(jnp.bfloat16)
    full_rows = lax.all_gather(normed, "mp", axis=1, tiled=True)
    image_count, tile_size, model_width = full_rows.shape
    head_count = weights_qkv.shape[1]
    joined_rows = jnp.dot(
        full_rows.reshape(image_count * tile_size, model_width),
        weights_qkv.reshape(model_width, -1),
        preferred_element_type=jnp.float32,
    )
    joined_rows = joined_rows.reshape(image_count, tile_size, head_count, GROUP + 2, HS)
    queries = rotate_half(joined_rows[:, :, :, :GROUP, :], angles[None, :, None, None, :]).astype(
        jnp.bfloat16
    )
    key_heads = rotate_half(joined_rows[:, :, :, GROUP, :], angles[None, :, None, :]).astype(
        jnp.bfloat16
    )
    value_heads = joined_rows[:, :, :, GROUP + 1, :].astype(jnp.bfloat16)
    score_scale = 1.0 / math.sqrt(HS)
    scores = (
        jnp.einsum("brhge,bche->bhgrc", queries, key_heads, preferred_element_type=jnp.float32)
        * score_scale
    )
    row_ids = jnp.arange(tile_size, dtype=jnp.int32)[:, None]
    col_ids = jnp.arange(tile_size, dtype=jnp.int32)[None, :]
    allowed = (col_ids <= row_ids)[None, None, None, :, :] & (
        col_ids[None, None, None, :, :] < lengths[:, None, None, None, None]
    )
    scores = jnp.where(allowed, scores, -1e30)
    row_max = jnp.max(scores, axis=-1, keepdims=True)
    weights = jnp.where(allowed, jnp.exp(scores - row_max), 0.0)
    probabilities = (weights / jnp.sum(weights, axis=-1, keepdims=True)).astype(jnp.bfloat16)
    attended = jnp.einsum(
        "bhgrc,bche->brhge", probabilities, value_heads, preferred_element_type=jnp.float32
    ).astype(jnp.bfloat16)
    head_term = jnp.dot(
        attended.reshape(image_count * tile_size, -1),
        weights_out.reshape(-1, model_width),
        preferred_element_type=jnp.float32,
    )
    head_term = head_term.reshape(image_count, tile_size, model_width)
    summed = lax.psum_scatter(
        head_term.astype(jnp.bfloat16), "mp", scatter_dimension=1, tiled=True
    ).astype(jnp.float32)
    return (as_float + summed).astype(jnp.bfloat16)


def body(
    vit_features,
    patch_counts,
    text_counts,
    tile_dest,
    text_embeds,
    w_proj,
    b_proj,
    norm_gain,
    w_qkv,
    w_out,
):
    rank_count = lax.axis_size("dp")
    my_rank = lax.axis_index("dp")
    image_count, local_rows, vision_width = vit_features.shape
    dest_ids = jnp.arange(rank_count, dtype=jnp.int32)
    own_hot = (tile_dest[:, None] == dest_ids[None, :]).astype(jnp.int32)
    own_before = jnp.sum((jnp.cumsum(own_hot, axis=0) - own_hot) * own_hot, axis=1)
    full_dest = collect(tile_dest, "dp", 0)
    full_slots = slot_table(full_dest, dest_ids)
    arrived = send_capped(
        vit_features, tile_dest, own_before, full_dest, full_slots, rank_count, my_rank
    )
    mp_rank = lax.axis_index("mp")
    projected = (
        jnp.dot(
            arrived.reshape(image_count * local_rows, vision_width),
            w_proj,
            preferred_element_type=jnp.float32,
        )
        + b_proj
    )
    projected = projected.reshape(image_count, local_rows, -1)
    row_ids = (mp_rank * local_rows + jnp.arange(local_rows, dtype=jnp.int32))[None, :, None]
    image_end = patch_counts[:, None, None]
    text_end = (patch_counts + text_counts)[:, None, None]
    hidden = jnp.where(
        row_ids < image_end,
        projected,
        jnp.where(row_ids < text_end, text_embeds.astype(jnp.float32), 0.0),
    ).astype(jnp.bfloat16)
    lengths = patch_counts + text_counts
    all_qkv, all_out = gather_turned((w_qkv, w_out), "dp", (1, 3))
    tile_size = local_rows * lax.axis_size("mp")
    angles = tile_angles(tile_size, HS)
    hidden = layer_step(hidden, norm_gain[0], all_qkv[0], all_out[0], lengths, angles)
    return hidden


def solution(mesh):
    in_specs = (
        P("dp", "mp", None),
        P("dp"),
        P("dp"),
        P("dp"),
        P("dp", "mp", None),
        P(),
        P(),
        P(),
        P(None, "dp", "mp", None),
        P(None, "mp", None, "dp"),
    )
    out_specs = P("dp", "mp", None)
    return jax.shard_map(body, mesh=mesh, in_specs=in_specs, out_specs=out_specs, check_vma=False)
```

profile of v0, /device:TPU:1, one launch (start us, length us, event | category | flops | bytes accessed | tf_op | source)
XLA Modules:
  0.0 328.6 jit_solution(4973166637287278460)
XLA Ops:
  6.5 1.0 copy.34
  7.6 1.5 pad_maximum_fusion
  9.1 1.3 broadcast_in_dim.37
  10.4 8.6 %all-to-all-start = ((s32[32,1,4]{2,1,0:T(1,128)}), s32[32,1,4]{2,1,0:T(1,128)S(1)}, u32[]{:S(2)}, u32[]{:S(2)}) async-start(s32[32,1,4]{2,1,0:T(1,128)} %broadcast_in_dim.37), calls=%async_computation | async-start | bytes 32768 | tf_op jit(solution)/shard_map/all_to_all | solution.py:16
  19.0 1.2 copy.47
  20.2 0.7 fusion.33
  20.9 0.8 select_reduce_fusion.1
  21.8 0.7 multiply_add_fusion
  22.4 1.4 convolution_convert_fusion
  23.8 4.4 %copy.48 = bf16[8,8,32,1024]{3,2,1,0:T(8,128)(2,1)} copy(bf16[8,8,32,1024]{3,1,2,0:T(8,128)(2,1)S(1)} %bitcast.93) | data formatting | bytes 8388608
  28.2 7.6 %all-to-all-start.1 = ((bf16[32,2,32,1024]{3,2,1,0:T(8,128)(2,1)}), bf16[32,2,32,1024]{3,2,1,0:T(8,128)(2,1)}, u32[]{:S(2)}, u32[]{:S(2)}) async-start(bf16[32,2,32,1024]{3,2,1,0:T(8,128)(2,1)} %bitcast.91), calls=%async_computation.1 | async-start | bytes 8388608 | tf_op jit(solution)/shard_map/all_to_all | solution.py:78
  36.5 0.7 reduce.5
  38.3 54.8 %all-to-all-done.1 = bf16[32,2,32,1024]{3,2,1,0:T(8,128)(2,1)} async-done(((bf16[32,2,32,1024]{3,2,1,0:T(8,128)(2,1)}), bf16[32,2,32,1024]{3,2,1,0:T(8,128)(2,1)}, u32[]{:S(2)}, u32[]{:S(2)}) %all-to-all-start.1) | async-done | bytes 4194336 | tf_op jit(solution)/shard_map/all_to_all | solution.py:78
  93.2 7.0 %copy.49 = bf16[8,8,32,1024]{3,1,2,0:T(8,128)(2,1)} copy(bf16[8,8,32,1024]{3,2,1,0:T(8,128)(2,1)} %bitcast.51) | data formatting | bytes 8388608
  100.1 3.2 convolution_convert_fusion.1
  103.5 4.7 %convolution_add_fusion = bf16[128,4096]{1,0:T(8,128)(2,1)S(1)} fusion(bf16[128,1024]{1,0:T(8,128)(2,1)S(1)} %reshape_reshape.3, bf16[1024,4096]{1,0:T(8,128)(2,1)} %param.15, f32[4096]{0:T(1024)S(1)} %copy-done.1), kind=kOutput, calls=%fused_computation.5 | convolution fusion | flops 1074790400 | bytes 9715712 | tf_op jit(solution)/shard_map/dot_general | solution.py:180
  109.0 1.3 fusion.4
  111.2 4.7 %slice.36 = bf16[4096,512]{0,1:T(8,128)(2,1)} slice(bf16[4096,768]{0,1:T(8,128)(2,1)} %all-gather.5.cloned.1.call-done), slice={[0:4096], [0:512]} | slice | bytes 8388608 | tf_op jit(solution)/shard_map/slice | solution.py:35
  115.9 92.3 %all-gather.3.cloned.1.call-done = bf16[4,256,4096]{2,1,0:T(8,128)(2,1)} async-done(((bf16[4,32,4096]{2,1,0:T(8,128)(2,1)}), bf16[4,256,4096]{2,1,0:T(8,128)(2,1)}) %all-gather.3.cloned.1.call-update) | async-done | bytes 8388624 | tf_op jit(solution)/shard_map/all_gather | solution.py:110
  208.2 8.2 %fusion.7 = f32[4,256,1,4,128]{1,4,3,0,2:T(8,128)S(1)} fusion(bf16[4,128,4096,1]{2,1,0,3:T(8,128)(2,1)} %bitcast.94, bf16[4,256,4096]{2,1,0:T(8,128)(2,1)} %all-gather.3.cloned.1.call-done), kind=kOutput, calls=%fused_computation.19 | convolution fusion | flops 4294967296 | bytes 14680064 | tf_op jit(solution)/shard_map/dot_general | solution.py:113
  217.8 0.8 convolution_convert_fusion.3
  218.6 7.2 %convolution_convert_fusion.2 = bf16[4,256,4096]{2,1,0:T(8,128)(2,1)} fusion(bf16[4,256,256]{1,2,0:T(8,128)(2,1)S(1)} %bitcast.96, bf16[4096,768]{0,1:T(8,128)(2,1)} %all-gather.5.cloned.1.call-done), kind=kOutput, calls=%fused_computation.4 | convolution fusion | flops 2151677952 | bytes 11010048 | tf_op jit(solution)/shard_map/dot_general | solution.py:143
  225.8 93.8 %reduce-scatter.2.cloned.1.call-done = bf16[4,32,4096]{2,1,0:T(8,128)(2,1)} async-done(((bf16[4,256,4096]{2,1,0:T(8,128)(2,1)}), bf16[4,32,4096]{2,1,0:T(8,128)(2,1)}) %reduce-scatter.2.cloned.1.call-update) | async-done | bytes 1048592 | tf_op jit(solution)/shard_map/reduce_scatter | solution.py:149
  319.6 2.4 fusion.5
  (46 shorter events, 4.9 us)
Async XLA Ops:
  6.5 104.7 %all-gather.5.cloned.1.call-start = ((), (), s32[]{:S(2)}) async-start(), calls=%async_computation.4 | async-start | bytes 6488064 | tf_op jit(solution)/shard_map/all_gather | solution.py:33
  10.4 17.8 %all-to-all-start = ((s32[32,1,4]{2,1,0:T(1,128)}), s32[32,1,4]{2,1,0:T(1,128)S(1)}, u32[]{:S(2)}, u32[]{:S(2)}) async-start(s32[32,1,4]{2,1,0:T(1,128)} %broadcast_in_dim.37), calls=%async_computation | async-start | bytes 32768 | tf_op jit(solution)/shard_map/all_to_all | solution.py:16
  28.2 7.6 %copy-start.3 = (s32[4]{0:T(128)S(1)}, s32[4]{0:T(128)}, u32[]{:S(2)}) copy-start(s32[4]{0:T(128)} %param.11) | copy-start | bytes 52
  28.2 7.6 %copy-start.4 = (s32[4]{0:T(128)S(1)}, s32[4]{0:T(128)}, u32[]{:S(2)}) copy-start(s32[4]{0:T(128)} %param.12) | copy-start | bytes 52
  28.2 64.9 %all-to-all-start.1 = ((bf16[32,2,32,1024]{3,2,1,0:T(8,128)(2,1)}), bf16[32,2,32,1024]{3,2,1,0:T(8,128)(2,1)}, u32[]{:S(2)}, u32[]{:S(2)}) async-start(bf16[32,2,32,1024]{3,2,1,0:T(8,128)(2,1)} %bitcast.91), calls=%async_computation.1 | async-start | bytes 8388608 | tf_op jit(solution)/shard_map/all_to_all | solution.py:78
  35.8 172.4 %all-gather.3.cloned.1.call-start = ((), (), s32[]{:S(2)}) async-start(), calls=%async_computation.3 | async-start | bytes 9437184 | tf_op jit(solution)/shard_map/all_gather | solution.py:110
  100.1 3.4 %copy-start.1 = (f32[4096]{0:T(1024)S(1)}, f32[4096]{0:T(1024)}, u32[]{:S(2)}) copy-start(f32[4096]{0:T(1024)} %param.16) | copy-start | bytes 49156
  103.5 4.8 %copy-start = (bf16[4,32,4096]{2,1,0:T(8,128)(2,1)S(1)}, bf16[4,32,4096]{2,1,0:T(8,128)(2,1)}, u32[]{:S(2)}) copy-start(bf16[4,32,4096]{2,1,0:T(8,128)(2,1)} %param.14) | copy-start | bytes 3145732
  108.3 0.7 copy-start.2
  110.3 209.3 %reduce-scatter.2.cloned.1.call-start = ((), (), s32[]{:S(2)}) async-start(), calls=%async_computation.5 | async-start | bytes 9437184 | tf_op jit(solution)/shard_map/reduce_scatter | solution.py:149
Sparse Core Ops, SparseCore 0:
  9.8 94.2 all-gather.4
  110.4 97.6 all-gather.2
  225.9 93.6 reduce-scatter.1
where the time goes:
time: 329 us
  waiting for transfers between devices  241 us (73%)
  matrix products  26 us (8%)
  local copies, waits for them, and re-layouts  20.7 us (6%)
  starting transfers between devices  16.4 us (5%)
  between operations  13.3 us (4%)
  other arithmetic  11.1 us (3%)
    reduce_scatter x1, waiting for transfers between devices, layer_step(): lax.psum_scatter(head_term.astype(jnp.bfloat16), 'mp', scatter_dimension=...  93.8 us
    all_gather x1, waiting for transfers between devices, layer_step(): full_rows = lax.all_gather(normed, 'mp', axis=1, tiled=True)  92.3 us
    all_to_all x1, waiting for transfers between devices, send_capped(): lax.all_to_all(outgoing, 'dp', split_axis=0, concat_axis=0, tiled=True)  54.8 us
    unnamed x14, local copies, waits for them, and re-layouts  13.7 us
    all_to_all x1, starting transfers between devices, sent_to_all(): return lax.all_to_all(copies, axis, split_axis=0, concat_axis=0, tiled=True)  8.58 us
    dot_general x1, matrix products, layer_step(): jnp.dot(full_rows.reshape(image_count * tile_size, model_width), weights_...  8.21 us
    all_to_all x1, starting transfers between devices, send_capped(): lax.all_to_all(outgoing, 'dp', split_axis=0, concat_axis=0, tiled=True)  7.57 us
    dot_general x1, matrix products, layer_step(): jnp.dot(attended.reshape(image_count * tile_size, -1), weights_out.reshap...  7.19 us
  transfers between devices with their start and end apart: 5, of which 3 were waited for; matrix products, arithmetic and copies ran while one was open for 11% of the time, Pallas kernels for 0%

commit v1 on v0

--- a/solution.py
+++ b/solution.py
@@ -9,6 +9,9 @@
 CAP = 2
 rope_base = 500000.0
 epsilon = 1e-05
+balance_cells = lambda matrix: jnp.concatenate(
+    lax.all_to_all(jnp.stack([matrix] * lax.axis_size("mp")), "mp", 0, 0), 1
+)
 
 
 def sent_to_all(shard, axis):
@@ -107,7 +110,7 @@
     as_float = hidden.astype(jnp.float32)
     mean_square = jnp.mean(as_float * as_float, axis=-1, keepdims=True)
     normed = (as_float * lax.rsqrt(mean_square + epsilon) * gain_row).astype(jnp.bfloat16)
-    full_rows = lax.all_gather(normed, "mp", axis=1, tiled=True)
+    full_rows = balance_cells(normed)
     image_count, tile_size, model_width = full_rows.shape
     head_count = weights_qkv.shape[1]
     joined_rows = jnp.dot(

time: 329 us -> 426 us (1.29)
  waiting for transfers between devices: 241 us -> 320 us
  local copies, waits for them, and re-layouts: 20.7 us -> 31.6 us
  starting transfers between devices: 16.4 us -> 24.8 us
    all_to_all x0 -> x1, waiting for transfers between devices: none -> 119 us  [lax.all_to_all(jnp.stack([matrix] * lax.axis_size('mp')), 'mp', 0, 0)]
    all_gather x1 -> x0, waiting for transfers between devices: 92.3 us -> none  [layer_step(): full_rows = lax.all_gather(normed, 'mp', axis=1, tiled=True)]
    all_gather x1, waiting for transfers between devices: 0.02 us -> 61.8 us  [gather_turned(): lax.all_gather(both, axis, axis=0, tiled=True)]
    all_to_all x0 -> x1, starting transfers between devices: none -> 8.32 us  [lax.all_to_all(jnp.stack([matrix] * lax.axis_size('mp')), 'mp', 0, 0)]
    reshape x0 -> x1, local copies, waits for them, and re-layouts: none -> 7.7 us  [jnp.concatenate(lax.all_to_all(jnp.stack([matrix] * lax.axis_size('mp')),...]
    all_to_all x1, waiting for transfers between devices: 54.8 us -> 49.7 us  [send_capped(): lax.all_to_all(outgoing, 'dp', split_axis=0, concat_axis=0, tiled=True)]
    unnamed x14 -> x18, local copies, waits for them, and re-layouts: 13.7 us -> 12.6 us
  transfers between devices with their start and end apart: 5 -> 5, of which waited for: 3 -> 4; matrix products, arithmetic and copies ran while one was open for 11% -> 4% of each run, Pallas kernels for 0% -> 0%
where the time goes in v1:
time: 426 us
  waiting for transfers between devices  320 us (75%)
  local copies, waits for them, and re-layouts  31.6 us (7%)
  matrix products  25.9 us (6%)
  starting transfers between devices  24.8 us (6%)
  between operations  13.7 us (3%)
  other arithmetic  9.23 us (2%)
    all_to_all x1, waiting for transfers between devices, lax.all_to_all(jnp.stack([matrix] * lax.axis_size('mp')), 'mp', 0, 0)  119 us
    reduce_scatter x1, waiting for transfers between devices, layer_step(): lax.psum_scatter(head_term.astype(jnp.bfloat16), 'mp', scatter_dimension=...  90.2 us
    all_gather x1, waiting for transfers between devices, gather_turned(): lax.all_gather(both, axis, axis=0, tiled=True)  61.8 us
    all_to_all x1, waiting for transfers between devices, send_capped(): lax.all_to_all(outgoing, 'dp', split_axis=0, concat_axis=0, tiled=True)  49.7 us
    unnamed x18, local copies, waits for them, and re-layouts  12.6 us
    all_to_all x1, starting transfers between devices, sent_to_all(): return lax.all_to_all(copies, axis, split_axis=0, concat_axis=0, tiled=True)  8.57 us
  transfers between devices with their start and end apart: 5, of which 4 were waited for; matrix products, arithmetic and copies ran while one was open for 4% of the time, Pallas kernels for 0%

profile of v1, /device:TPU:1, one launch (start us, length us, event | category | flops | bytes accessed | tf_op | source)
XLA Modules:
  0.0 425.6 jit_solution(8515496710684595112)
XLA Ops:
  6.5 1.3 broadcast_in_dim.37
  7.8 8.6 %all-to-all-start = ((s32[32,1,4]{2,1,0:T(1,128)}), s32[32,1,4]{2,1,0:T(1,128)S(1)}, u32[]{:S(2)}, u32[]{:S(2)}) async-start(s32[32,1,4]{2,1,0:T(1,128)} %broadcast_in_dim.37), calls=%async_computation | async-start | bytes 32768 | tf_op jit(solution)/shard_map/all_to_all | solution.py:19
  16.4 0.7 fusion.28
  17.1 1.2 copy.49
  18.3 0.8 select_reduce_fusion.1
  19.8 1.4 convolution_convert_fusion
  21.2 4.4 %copy.50 = bf16[8,8,32,1024]{3,2,1,0:T(8,128)(2,1)} copy(bf16[8,8,32,1024]{3,1,2,0:T(8,128)(2,1)S(1)} %bitcast.93) | data formatting | bytes 8388608
  25.6 7.6 %all-to-all-start.1 = ((bf16[32,2,32,1024]{3,2,1,0:T(8,128)(2,1)}), bf16[32,2,32,1024]{3,2,1,0:T(8,128)(2,1)}, u32[]{:S(2)}, u32[]{:S(2)}) async-start(bf16[32,2,32,1024]{3,2,1,0:T(8,128)(2,1)} %bitcast.91), calls=%async_computation.1 | async-start | bytes 8388608 | tf_op jit(solution)/shard_map/all_to_all | solution.py:81
  35.7 49.7 %all-to-all-done.1 = bf16[32,2,32,1024]{3,2,1,0:T(8,128)(2,1)} async-done(((bf16[32,2,32,1024]{3,2,1,0:T(8,128)(2,1)}), bf16[32,2,32,1024]{3,2,1,0:T(8,128)(2,1)}, u32[]{:S(2)}, u32[]{:S(2)}) %all-to-all-start.1) | async-done | bytes 4194336 | tf_op jit(solution)/shard_map/all_to_all | solution.py:81
  85.3 6.8 %copy.51 = bf16[8,8,32,1024]{3,1,2,0:T(8,128)(2,1)} copy(bf16[8,8,32,1024]{3,2,1,0:T(8,128)(2,1)} %bitcast.54) | data formatting | bytes 8388608
  92.1 3.0 convolution_convert_fusion.1
  95.4 4.7 %convolution_add_fusion = bf16[128,4096]{1,0:T(8,128)(2,1)S(1)} fusion(bf16[128,1024]{1,0:T(8,128)(2,1)S(1)} %reshape_reshape.4, bf16[1024,4096]{1,0:T(8,128)(2,1)} %param.15, f32[4096]{0:T(1024)S(1)} %copy-done.3), kind=kOutput, calls=%fused_computation.3 | convolution fusion | flops 1074790400 | bytes 9715712 | tf_op jit(solution)/shard_map/dot_general | solution.py:183
  101.2 4.3 stack.2
  105.4 8.3 %all-to-all-start.2 = ((bf16[8,4,32,4096]{3,2,1,0:T(8,128)(2,1)}), bf16[8,4,32,4096]{3,2,1,0:T(8,128)(2,1)}, u32[]{:S(2)}, u32[]{:S(2)}) async-start(bf16[8,4,32,4096]{3,2,1,0:T(8,128)(2,1)} %stack.2), calls=%async_computation.2 | async-start | bytes 16777216 | tf_op jit(solution)/shard_map/all_to_all | solution.py:13
  113.9 0.7 pad_maximum_fusion
  115.6 61.8 %all-gather.2.cloned.1.call-done = bf16[4096,768]{0,1:T(8,128)(2,1)} async-done(((bf16[128,768]{0,1:T(8,128)(2,1)}), bf16[4096,768]{0,1:T(8,128)(2,1)}) %all-gather.2.cloned.1.call-update) | async-done | bytes 6291472 | tf_op jit(solution)/shard_map/all_gather | solution.py:36
  177.3 4.7 %slice.36 = bf16[4096,512]{0,1:T(8,128)(2,1)} slice(bf16[4096,768]{0,1:T(8,128)(2,1)} %all-gather.2.cloned.1.call-done), slice={[0:4096], [0:512]} | slice | bytes 8388608 | tf_op jit(solution)/shard_map/slice | solution.py:38
  182.0 118.8 %all-to-all-done.2 = bf16[8,4,32,4096]{3,2,1,0:T(8,128)(2,1)} async-done(((bf16[8,4,32,4096]{3,2,1,0:T(8,128)(2,1)}), bf16[8,4,32,4096]{3,2,1,0:T(8,128)(2,1)}, u32[]{:S(2)}, u32[]{:S(2)}) %all-to-all-start.2) | async-done | bytes 8388640 | tf_op jit(solution)/shard_map/all_to_all | solution.py:13
  300.8 7.7 %copy.35 = bf16[4,8,32,4096]{3,2,1,0:T(8,128)(2,1)} copy(bf16[4,8,32,4096]{3,2,0,1:T(8,128)(2,1)} %bitcast.3) | data formatting | bytes 16777216 | tf_op jit(solution)/shard_map/reshape | solution.py:12
  308.5 8.2 %convolution_bitcast_fusion = f32[4,256,1,4,128]{1,4,3,0,2:T(8,128)S(1)} fusion(bf16[4,256,4096,1]{2,1,3,0:T(8,128)(2,1)} %bitcast.94, bf16[4,128,4096,1]{2,1,0,3:T(8,128)(2,1)} %bitcast.95), kind=kOutput, calls=%fused_computation.17 | convolution fusion | flops 4294967296 | bytes 14680064 | tf_op jit(solution)/shard_map/dot_general | solution.py:116
  318.1 0.8 convolution_convert_fusion.3
  318.9 7.2 %convolution_convert_fusion.2 = bf16[4,256,4096]{2,1,0:T(8,128)(2,1)} fusion(bf16[4,256,256]{1,2,0:T(8,128)(2,1)S(1)} %bitcast.97, bf16[4096,768]{0,1:T(8,128)(2,1)} %all-gather.2.cloned.1.call-done), kind=kOutput, calls=%fused_computation.2 | convolution fusion | flops 2151677952 | bytes 11010048 | tf_op jit(solution)/shard_map/dot_general | solution.py:146
  326.1 90.2 %reduce-scatter.2.cloned.1.call-done = bf16[4,32,4096]{2,1,0:T(8,128)(2,1)} async-done(((bf16[4,256,4096]{2,1,0:T(8,128)(2,1)}), bf16[4,32,4096]{2,1,0:T(8,128)(2,1)}) %reduce-scatter.2.cloned.1.call-update) | async-done | bytes 1048592 | tf_op jit(solution)/shard_map/reduce_scatter | solution.py:152
  416.3 2.4 fusion.3
  (51 shorter events, 6.7 us)
Async XLA Ops:
  7.8 17.8 %all-to-all-start = ((s32[32,1,4]{2,1,0:T(1,128)}), s32[32,1,4]{2,1,0:T(1,128)S(1)}, u32[]{:S(2)}, u32[]{:S(2)}) async-start(s32[32,1,4]{2,1,0:T(1,128)} %broadcast_in_dim.37), calls=%async_computation | async-start | bytes 32768 | tf_op jit(solution)/shard_map/all_to_all | solution.py:19
  25.6 7.6 %copy-start.5 = (s32[4]{0:T(128)S(1)}, s32[4]{0:T(128)}, u32[]{:S(2)}) copy-start(s32[4]{0:T(128)} %param.11) | copy-start | bytes 52
  25.6 7.6 %copy-start.6 = (s32[4]{0:T(128)S(1)}, s32[4]{0:T(128)}, u32[]{:S(2)}) copy-start(s32[4]{0:T(128)} %param.12) | copy-start | bytes 52
  25.6 59.7 %all-to-all-start.1 = ((bf16[32,2,32,1024]{3,2,1,0:T(8,128)(2,1)}), bf16[32,2,32,1024]{3,2,1,0:T(8,128)(2,1)}, u32[]{:S(2)}, u32[]{:S(2)}) async-start(bf16[32,2,32,1024]{3,2,1,0:T(8,128)(2,1)} %bitcast.91), calls=%async_computation.1 | async-start | bytes 8388608 | tf_op jit(solution)/shard_map/all_to_all | solution.py:81
  92.1 3.3 copy-start.3
  95.3 4.8 %copy-start = (bf16[4,32,4096]{2,1,0:T(8,128)(2,1)S(1)}, bf16[4,32,4096]{2,1,0:T(8,128)(2,1)}, u32[]{:S(2)}) copy-start(bf16[4,32,4096]{2,1,0:T(8,128)(2,1)} %param.14) | copy-start | bytes 3145732
  100.1 0.7 copy-start.4
  105.4 8.4 %copy-start.1 = (bf16[1,128,1,512]{3,1,2,0:T(8,128)(2,1)S(1)}, bf16[1,128,1,512]{3,1,2,0:T(8,128)(2,1)}, u32[]{:S(2)}) copy-start(bf16[1,128,1,512]{3,1,2,0:T(8,128)(2,1)} %param.18) | copy-start | bytes 393220
  105.4 8.5 %copy-start.2 = (bf16[1,1,256,128]{3,2,1,0:T(8,128)(2,1)S(1)}, bf16[1,1,256,128]{3,2,1,0:T(8,128)(2,1)}, u32[]{:S(2)}) copy-start(bf16[1,1,256,128]{3,2,1,0:T(8,128)(2,1)} %param.19) | copy-start | bytes 196612
  105.4 195.4 %all-to-all-start.2 = ((bf16[8,4,32,4096]{3,2,1,0:T(8,128)(2,1)}), bf16[8,4,32,4096]{3,2,1,0:T(8,128)(2,1)}, u32[]{:S(2)}, u32[]{:S(2)}) async-start(bf16[8,4,32,4096]{3,2,1,0:T(8,128)(2,1)} %stack.2), calls=%async_computation.2 | async-start | bytes 16777216 | tf_op jit(solution)/shard_map/all_to_all | solution.py:13
  113.7 63.6 %all-gather.2.cloned.1.call-start = ((), (), s32[]{:S(2)}) async-start(), calls=%async_computation.4 | async-start | bytes 6488064 | tf_op jit(solution)/shard_map/all_gather | solution.py:36
  114.6 301.6 %reduce-scatter.2.cloned.1.call-start = ((), (), s32[]{:S(2)}) async-start(), calls=%async_computation.5 | async-start | bytes 9437184 | tf_op jit(solution)/shard_map/reduce_scatter | solution.py:152
Sparse Core Ops, SparseCore 0:
  117.0 60.2 all-gather.1
  326.2 89.9 reduce-scatter.1
